TPU v7x, 32 devices: a 4x2x2 block of a 4x4x8 slice. The times are simulated.
32 devices in a mesh: batch: 4 (over y, z), time: 8 (over x, core).
Axes of the slice: x: 4, y: 2, z: 2, core: 2. Of those that a mesh axis runs over, the one named last changes fastest.
The devices are a block of a 4x4x8 slice.
Arguments:
- latent: bfloat16 [64, 6, 128, 384], P(('batch', 'time')), parts along dimension 0
- conv_w: bfloat16 [4, 3, 3, 3, 384, 384], replicated
- conv_b: float32 [4, 384], replicated
- norm_g: float32 [5, 384], replicated
- norm_b: float32 [5, 384], replicated
- attn_w: bfloat16 [4, 384, 384], replicated
- attn_b: float32 [4, 384], replicated
Outputs:
- output: bfloat16 [64, 6, 128, 384], P(('batch', 'time')), parts along dimension 0
There are 4 independent parts. A program takes and returns all parts, laid end to end along the dimension named above; an argument that names none is the same for every part.
All inputs are finite; a program needn't handle non-finite values.
Results may differ from a plain program's by a relative error of at most 0.0124883.
Values are sent between devices in bfloat16 or wider.
A program may use at most 768 MiB of HBM per device.

v0:
```python
import functools

import jax
import jax.numpy as jnp
from jax import lax
from jax.experimental import pallas as pl
from jax.experimental.pallas import tpu as pltpu
from jax.sharding import PartitionSpec as P

GROUPS = 32
NORM_EPS = 1e-6
CHUNK = 64
MESH = pl.DeviceIdType.MESH
F32 = jnp.float32
BF16 = jnp.bfloat16


def dot_t(lhs, rhs):
    return lax.dot_general(lhs, rhs, (((0,), (0,)), ((), ())), preferred_element_type=F32)


def kernel(ranks, height, width, x_hbm, w_hbm, conv_b, norm_g, norm_b, attn_w, attn_b, out_ref,
           x_in, w_buf, u_buf, acc, feat, halo, part, stat, coef, attn_q, attn_k, attn_v, attn_p,
           x_sem, w_sem, stat_send, stat_recv, halo_send, halo_recv):
    me = lax.axis_index("time")
    channels = feat.shape[2]
    per_group = channels // GROUPS
    elem_count = float(ranks * 2 * height * width * per_group)
    npos = height * width
    nchunk = channels // CHUNK
    k_tap = 3 * channels

    def x_copy():
        return pltpu.make_async_copy(x_hbm, x_in, x_sem)

    def w_copy(k, a):
        return pltpu.make_async_copy(w_hbm.at[k, a], w_buf.at[k % 2, a], w_sem.at[k % 2, a])

    def stat_copy(n, source, target):
        return pltpu.make_async_remote_copy(
            src_ref=stat.at[n, source], dst_ref=stat.at[n, source], send_sem=stat_send.at[n, target],
            recv_sem=stat_recv.at[n, source], device_id={"time": target}, device_id_type=MESH)

    def halo_copy(k, t):
        return pltpu.make_async_remote_copy(
            src_ref=feat.at[k % 2, t], dst_ref=halo.at[k, t], send_sem=halo_send.at[k, t],
            recv_sem=halo_recv.at[k, t], device_id={"time": lax.rem(me + 1, ranks)}, device_id_type=MESH)

    def start_halo(k):
        @pl.when(me < ranks - 1)
        def _():
            for t in (1, 0):
                halo_copy(k, t).start()

    def send_stats(n):
        rows = [jnp.sum(part[i].T, axis=0, keepdims=True) for i in range(2)]
        stat[n, me] = jnp.concatenate(rows, axis=0)
        for d in range(1, ranks):
            stat_copy(n, me, lax.rem(me + d, ranks)).start()

    def column(row):
        return jnp.broadcast_to(row, (128, channels)).T

    def norm_coefs(n):
        for d in range(1, ranks):
            stat_copy(n, lax.rem(me + d, ranks), lax.rem(me + d, ranks)).wait_recv()
        totals = jnp.sum(stat[n], axis=0)
        totals = jnp.concatenate([totals, jnp.zeros((6, channels), F32)], axis=0)
        magic = (65536 + per_group - 1) // per_group
        r = lax.broadcasted_iota(jnp.int32, (channels, channels), 0) * magic // 65536
        c = lax.broadcasted_iota(jnp.int32, (channels, channels), 1) * magic // 65536
        member = jnp.where(r == c, 1.0, 0.0).astype(F32)
        sums = jnp.dot(totals, member, precision=lax.Precision.HIGHEST, preferred_element_type=F32)
        mean = sums[0:1] / elem_count
        var = sums[1:2] / elem_count - mean * mean
        scale = lax.rsqrt(var + NORM_EPS) * norm_g[pl.ds(n, 1), :]
        coef[0] = column(mean)
        coef[1] = column(scale)
        coef[2] = column(norm_b[pl.ds(n, 1), :])
        for d in range(1, ranks):
            stat_copy(n, me, lax.rem(me + d, ranks)).wait_send()

    def normalize(value, c0):
        sl = pl.ds(c0, CHUNK)
        return (value.astype(F32) - coef[0, sl, :]) * coef[1, sl, :] + coef[2, sl, :]

    def fill_u(read, s):
        lane = lax.broadcasted_iota(jnp.int32, (CHUNK, width), 1)

        def body(ci, _):
            c0 = pl.multiple_of(ci * CHUNK, CHUNK)
            for i in range(height):
                half = 0.5 * normalize(read(c0, i), c0)
                u = half + half * jnp.tanh(half)
                left = jnp.where(lane == 0, 0.0, pltpu.roll(u, 1, 1))
                right = jnp.where(lane == width - 1, 0.0, pltpu.roll(u, width - 1, 1))
                cols = pl.ds((i + 1) * width, width)
                for e, v in enumerate((left, u, right)):
                    u_buf[s, pl.ds(e * channels + c0, CHUNK), cols] = v.astype(BF16)
            return 0

        lax.fori_loop(0, nchunk, body, 0)

    def taps(s):
        return jnp.concatenate([u_buf[s, :, pl.ds(d * width, npos)] for d in range(3)], axis=0)

    def frame_read(b, t):
        return lambda c0, i: feat[b, t, pl.ds(c0, CHUNK), pl.ds(i * width, width)]

    def halo_read(k, t):
        return lambda c0, i: halo[k, t, pl.ds(c0, CHUNK), pl.ds(i * width, width)]

    def get_halo(k, t):
        @pl.when(me > 0)
        def _():
            halo_copy(k, t).wait_recv()

        @pl.when(me == 0)
        def _():
            halo[k, t] = feat[k % 2, 0]

        fill_u(halo_read(k, t), t)

    def accumulate_stats(value_of):
        def body(ci, _):
            c0 = pl.multiple_of(ci * CHUNK, CHUNK)
            s1 = jnp.zeros((CHUNK, width), F32)
            s2 = jnp.zeros((CHUNK, width), F32)
            for t in range(2):
                for i in range(height):
                    v = value_of(t, c0, i)
                    s1 = s1 + v
                    s2 = s2 + v * v
            part[0, pl.ds(c0, CHUNK), :] = s1
            part[1, pl.ds(c0, CHUNK), :] = s2
            return 0

        lax.fori_loop(0, nchunk, body, 0)

    def attention():
        def norm_body(ci, _):
            c0 = pl.multiple_of(ci * CHUNK, CHUNK)
            for t in range(2):
                for i in range(height):
                    a = normalize(feat[0, t, pl.ds(c0, CHUNK), pl.ds(i * width, width)], c0)
                    u_buf[t, pl.ds(c0, CHUNK), pl.ds((i + 1) * width, width)] = a.astype(BF16)
            return 0

        lax.fori_loop(0, nchunk, norm_body, 0)
        for j in range(4):
            acc[j // 2, :, pl.ds((j % 2) * 128, 128)] = column(attn_b[j:j + 1, :])

        def bias(j):
            return jnp.concatenate([acc[j // 2, :, pl.ds((j % 2) * 128, 128)]] * height, axis=1)

        def frame(t, _):
            a = u_buf[t, pl.ds(0, channels), pl.ds(width, npos)]
            for j, ref in enumerate((attn_q, attn_k, attn_v)):
                ref[...] = (dot_t(attn_w[j], a) + bias(j)).astype(BF16)
            block = 256
            for qb in range(npos // block):
                cols = pl.ds(qb * block, block)
                s = dot_t(attn_k[...], attn_q[:, cols]) * channels ** -0.5
                p = jnp.exp(s - jnp.max(s, axis=0, keepdims=True))
                attn_p[:, cols] = (p * (1.0 / jnp.sum(p, axis=0, keepdims=True))).astype(BF16)
            attn_q[...] = jnp.dot(attn_v[...], attn_p[...], preferred_element_type=F32).astype(BF16)
            o = (dot_t(attn_w[3], attn_q[...]) + bias(3)).astype(BF16)
            feat[0, t] = (feat[0, t].astype(F32) + o.astype(F32)).astype(BF16)
            return 0

        lax.fori_loop(0, 2, frame, 0)

    x_copy().start()
    for a in (2, 1, 0):
        w_copy(0, a).start()
    barrier = pltpu.get_barrier_semaphore()
    for d in range(1, ranks):
        pl.semaphore_signal(barrier, inc=1, device_id={"time": lax.rem(me + d, ranks)}, device_id_type=MESH)
    for a in (2, 1, 0):
        w_copy(1, a).start()
    for s in range(4):
        for row in (0, height + 1):
            u_buf[s, :, pl.ds(row * width, width)] = jnp.zeros((k_tap, width), BF16)
    x_copy().wait()
    for t in range(2):
        feat[0, t] = x_in[t].T

    def plain_value(t, c0, i):
        return feat[0, t, pl.ds(c0, CHUNK), pl.ds(i * width, width)].astype(F32)

    accumulate_stats(plain_value)
    pl.semaphore_wait(barrier, ranks - 1)
    send_stats(0)
    start_halo(0)

    def conv_stage(k, _):
        src = k % 2
        dst = 1 - src
        n = k + k // 2
        slot = k % 2
        norm_coefs(n)
        for t in range(2):
            fill_u(frame_read(src, t), 2 + t)
        for a in (2, 1):
            w_copy(k, a).wait()
        acc[1] = dot_t(jnp.concatenate([w_buf[slot, 1], w_buf[slot, 2]], axis=0),
                       jnp.concatenate([taps(2), taps(3)], axis=0))
        acc[0] = dot_t(w_buf[slot, 2], taps(2))
        w_copy(k, 0).wait()
        get_halo(k, 1)
        acc[1] = acc[1] + dot_t(w_buf[slot, 0], taps(1))
        acc[0] = acc[0] + dot_t(w_buf[slot, 1], taps(1))
        get_halo(k, 0)
        acc[0] = acc[0] + dot_t(w_buf[slot, 0], taps(0))

        @pl.when(k < 2)
        def _():
            for a in (2, 1, 0):
                w_copy(k + 2, a).start()

        @pl.when(me < ranks - 1)
        def _():
            for t in (1, 0):
                halo_copy(k, t).wait_send()

        coef[0] = column(conv_b[pl.ds(k, 1), :])
        odd = src == 1

        def conv_value(t, c0, i):
            rows, cols = pl.ds(c0, CHUNK), pl.ds(i * width, width)
            h = (acc[t, rows, cols] + coef[0, rows, :]).astype(BF16).astype(F32)
            res = (feat[0, t, rows, cols].astype(F32) + h)
            y = jnp.where(odd, res, h).astype(BF16)
            feat[dst, t, rows, cols] = y
            return y.astype(F32)

        accumulate_stats(conv_value)

        @pl.when(k < 3)
        def _():
            send_stats(n + 1)

        @pl.when(src == 0)
        def _():
            start_halo(k + 1)

        @pl.when(k == 1)
        def _():
            norm_coefs(2)
            attention()
            accumulate_stats(plain_value)
            send_stats(3)
            start_halo(2)

        return 0

    lax.fori_loop(0, 4, conv_stage, 0)
    for t in range(2):
        out_ref[t] = feat[0, t].T


def solution(mesh):
    ranks = mesh.shape["time"]
    video_spec = P(("batch", "time"), None, None, None)

    def device_body(latent, conv_w, conv_b, norm_g, norm_b, attn_w, attn_b):
        frames, height, width, channels = latent.shape
        npos = height * width
        vmem = pl.BlockSpec(memory_space=pltpu.VMEM)
        hbm = pl.BlockSpec(memory_space=pl.ANY)
        dma = pltpu.SemaphoreType.DMA
        out = pl.pallas_call(
            functools.partial(kernel, ranks, height, width),
            out_shape=jax.ShapeDtypeStruct((frames, npos, channels), BF16),
            in_specs=[hbm, hbm] + [vmem] * 5,
            out_specs=vmem,
            scratch_shapes=[
                pltpu.VMEM((frames, npos, channels), BF16),
                pltpu.VMEM((2, 3, 9 * channels, channels), BF16),
                pltpu.VMEM((4, 3 * channels, (height + 2) * width), BF16),
                pltpu.VMEM((2, channels, npos), F32),
                pltpu.VMEM((2, 2, channels, npos), BF16),
                pltpu.VMEM((4, 2, channels, npos), BF16),
                pltpu.VMEM((2, channels, 128), F32),
                pltpu.VMEM((5, ranks, 2, channels), F32),
                pltpu.VMEM((3, channels, 128), F32),
                pltpu.VMEM((channels, npos), BF16),
                pltpu.VMEM((channels, npos), BF16),
                pltpu.VMEM((channels, npos), BF16),
                pltpu.VMEM((npos, npos), BF16),
                dma(()), dma((2, 3)), dma((5, ranks)), dma((5, ranks)), dma((4, 2)), dma((4, 2)),
            ],
            compiler_params=pltpu.CompilerParams(
                collective_id=0, has_side_effects=True, vmem_limit_bytes=62 * 2 ** 20),
            name="mid_block",
        )(latent.reshape(frames, npos, channels), conv_w.reshape(4, 3, 9 * channels, channels),
          conv_b, norm_g, norm_b, attn_w, attn_b)
        return out.reshape(latent.shape)

    return jax.shard_map(device_body, mesh=mesh, in_specs=(video_spec, P(), P(), P(), P(), P(), P()),
                         out_specs=video_spec, check_vma=False)
```

profile of v0, /device:TPU:81, one launch (start us, length us, event | category | flops | bytes accessed | tf_op | source)
XLA Modules:
  0.0 118.7 jit_solution(16354417109253407081)
XLA Ops:
  0.0 116.3 %mid_block.1 = bf16[2,768,384]{2,1,0:T(8,128)(2,1)} custom-call(bf16[2,768,384]{2,1,0:T(8,128)(2,1)} %bitcast.5, bf16[4,3,3456,384]{3,2,1,0:T(8,128)(2,1)} %bitcast.3, f32[4,384]{1,0:T(4,128)} %conv_b.1, f32[5,384]{1,0:T(8,128)} %norm_g.1, f32[5,384]{1,0:T(8,128)} %norm_b.1, bf16[4,384,384]{2,1,0:T(8,128)(2,1)} %attn_w.1, f32[4,384]{1,0:T(4,128)} %attn_b.1), custom_call_target="tpu_custom_call" | custom-call | tf_op jit(solution)/shard_map/mid_block/pallas_call | solution.py:272
  116.3 2.4 %copy.9 = bf16[2,6,128,384]{3,2,1,0:T(8,128)(2,1)} copy(bf16[2,6,128,384]{3,2,1,0:T(8,128)(2,1)} %bitcast.4) | data formatting | bytes 2359296
where the time goes:
time: 119 us
  Pallas kernels  116 us (97%)
  local copies, waits for them, and re-layouts  2.41 us (2%)
    pallas_call x1, Pallas kernels, device_body(): pl.pallas_call(functools.partial(kernel, ranks, height, width), out_shape...  116 us
    unnamed x1, local copies, waits for them, and re-layouts  2.41 us

commit v1 on v0

v1 whole, which is shorter than its diff:
```python
import functools

import jax
import jax.numpy as jnp
from jax import lax
from jax.experimental import pallas as pl
from jax.experimental.pallas import tpu as pltpu
from jax.sharding import PartitionSpec as P

GROUPS = 32
NORM_EPS = 1e-6
CHUNK = 64
WIDE = 128
MESH = pl.DeviceIdType.MESH
F32 = jnp.float32
BF16 = jnp.bfloat16


def dot_t(lhs, rhs):
    return lax.dot_general(lhs, rhs, (((0,), (0,)), ((), ())), preferred_element_type=F32)


def kernel(ranks, height, width, x_hbm, w_hbm, conv_b, norm_g, norm_b, attn_w, attn_b, out_ref,
           x_in, w_buf, u_0, u_1, u_2, u_3, acc, feat, xres, halo, part, stat, coef, bias_col, member,
           attn_a, attn_q, attn_k, attn_v, attn_p,
           x_sem, w_sem, stat_send, stat_recv, halo_send, halo_recv):
    me = lax.axis_index("time")
    channels = feat.shape[3]
    u_bufs = (u_0, u_1, u_2, u_3)
    per_group = channels // GROUPS
    elem_count = float(ranks * 2 * height * width * per_group)
    npos = height * width
    nchunk = channels // CHUNK
    k_tap = 3 * channels

    def x_copy():
        return pltpu.make_async_copy(x_hbm, x_in, x_sem)

    def w_copy(k, a):
        return [pltpu.make_async_copy(w_hbm.at[k, a, :, pl.ds(j * 128, 128)], w_buf.at[k % 2, a, j],
                                      w_sem.at[k % 2, a, j]) for j in range(channels // 128)]

    def start_weights(k):
        for a in (2, 1, 0):
            for copy in w_copy(k, a):
                copy.start()

    def wait_weights(k, a):
        for copy in w_copy(k, a):
            copy.wait()

    def weights(slot, *taps_in_time):
        return jnp.concatenate([jnp.concatenate([w_buf[slot, a, j] for j in range(channels // 128)], axis=1)
                                for a in taps_in_time], axis=0)

    def wide(read):
        return jnp.concatenate([read(i) for i in range(height)], axis=1)

    def put(ref, value):
        for i in range(height):
            ref[i] = value[:, i * width:(i + 1) * width]

    def stat_copy(n, source, target):
        return pltpu.make_async_remote_copy(
            src_ref=stat.at[n, source], dst_ref=stat.at[n, source], send_sem=stat_send.at[n, target],
            recv_sem=stat_recv.at[n, source], device_id={"time": target}, device_id_type=MESH)

    def halo_copy(k, t):
        return pltpu.make_async_remote_copy(
            src_ref=feat.at[k % 2, t], dst_ref=halo.at[k, t], send_sem=halo_send.at[k, t],
            recv_sem=halo_recv.at[k, t], device_id={"time": lax.rem(me + 1, ranks)}, device_id_type=MESH)

    def start_halo(k):
        @pl.when(me < ranks - 1)
        def _():
            for t in (1, 0):
                halo_copy(k, t).start()

    def send_stats(n):
        rows = [jnp.sum(part[i].T, axis=0, keepdims=True) for i in range(2)]
        stat[n, me] = jnp.concatenate(rows, axis=0)
        for d in range(1, ranks):
            stat_copy(n, me, lax.rem(me + d, ranks)).start()

    def column(row):
        return jnp.broadcast_to(row, (128, channels)).T

    def norm_coefs(n):
        coef[2] = column(norm_b[pl.ds(n, 1), :])
        for d in range(1, ranks):
            stat_copy(n, lax.rem(me + d, ranks), lax.rem(me + d, ranks)).wait_recv()
        totals = jnp.sum(stat[n], axis=0)
        totals = jnp.concatenate([totals, jnp.zeros((6, channels), F32)], axis=0)
        high = totals.astype(BF16).astype(F32)
        rest = totals - high
        mid = rest.astype(BF16).astype(F32)
        low = rest - mid
        parts = jnp.concatenate([high, mid, low, jnp.zeros_like(low)], axis=0).astype(BF16)
        sums = jnp.dot(parts, member[...], preferred_element_type=F32)
        sums = sums[0:8] + sums[8:16] + sums[16:24]
        mean = sums[0:1] / elem_count
        var = sums[1:2] / elem_count - mean * mean
        scale = lax.rsqrt(var + NORM_EPS) * norm_g[pl.ds(n, 1), :]
        coef[0] = column(mean)
        coef[1] = column(scale)
        for d in range(1, ranks):
            stat_copy(n, me, lax.rem(me + d, ranks)).wait_send()

    def normalize(value, c0, size=CHUNK):
        sl = pl.ds(c0, size)
        return (value.astype(F32) - coef[0, sl, :]) * coef[1, sl, :] + coef[2, sl, :]

    def fill_rows(read, s, c0, size):
        lane = lax.broadcasted_iota(jnp.int32, (size, width), 1)
        for i in range(height):
            half = 0.5 * normalize(read(c0, size, i), c0, size)
            u = (half + half * jnp.tanh(half)).astype(BF16)
            left = jnp.where(lane == 0, jnp.zeros_like(u), pltpu.roll(u, 1, 1))
            right = jnp.where(lane == width - 1, jnp.zeros_like(u), pltpu.roll(u, width - 1, 1))
            for e, v in enumerate((left, u, right)):
                u_bufs[s][i + 1, pl.ds(e * channels + c0, size), :] = v

    def fill_u(read, s):
        def body(ci, _):
            fill_rows(read, s, pl.multiple_of(ci * WIDE, WIDE), WIDE)
            return 0

        lax.fori_loop(0, channels // WIDE, body, 0)

    def taps(s):
        return jnp.concatenate([wide(lambda i: u_bufs[s][d + i]) for d in range(3)], axis=0)

    def frame_read(b, t):
        return lambda c0, size, i: feat[b, t, i, pl.ds(c0, size), :]

    def halo_read(k, t):
        return lambda c0, size, i: halo[k, t, i, pl.ds(c0, size), :]

    def get_halo(k, t):
        @pl.when(me > 0)
        def _():
            halo_copy(k, t).wait_recv()

        @pl.when(me == 0)
        def _():
            halo[k, t] = feat[k % 2, 0]

        fill_u(halo_read(k, t), t)

    def accumulate_stats(value_of):
        def body(ci, _):
            c0 = pl.multiple_of(ci * CHUNK, CHUNK)
            s1 = jnp.zeros((CHUNK, width), F32)
            s2 = jnp.zeros((CHUNK, width), F32)
            for t in range(2):
                for i in range(height):
                    v = value_of(t, c0, i)
                    s1 = s1 + v
                    s2 = s2 + v * v
            part[0, pl.ds(c0, CHUNK), :] = s1
            part[1, pl.ds(c0, CHUNK), :] = s2
            return 0

        lax.fori_loop(0, nchunk, body, 0)

    def attention():
        def norm_body(ci, _):
            c0 = pl.multiple_of(ci * CHUNK, CHUNK)
            for t in range(2):
                for i in range(height):
                    a = normalize(feat[0, t, i, pl.ds(c0, CHUNK), :], c0)
                    attn_a[t, i, pl.ds(c0, CHUNK), :] = a.astype(BF16)
            return 0

        lax.fori_loop(0, nchunk, norm_body, 0)
        for j in range(4):
            acc[0, j] = column(attn_b[j:j + 1, :])

        def bias(j):
            return jnp.concatenate([acc[0, j]] * height, axis=1)

        def frame(t, _):
            a = wide(lambda i: attn_a[t, i])
            for j, ref in enumerate((attn_q, attn_k, attn_v)):
                put(ref, (dot_t(attn_w[j], a) + bias(j)).astype(BF16))
            keys = wide(lambda i: attn_k[i])
            for qb in range(height // 2):
                query = jnp.concatenate([attn_q[2 * qb], attn_q[2 * qb + 1]], axis=1)
                s = dot_t(keys, query) * channels ** -0.5
                p = jnp.exp(s - jnp.max(s, axis=0, keepdims=True))
                p = (p * (1.0 / jnp.sum(p, axis=0, keepdims=True))).astype(BF16)
                attn_p[2 * qb] = p[:, :width]
                attn_p[2 * qb + 1] = p[:, width:]
            mixed = jnp.dot(wide(lambda i: attn_v[i]), wide(lambda i: attn_p[i]), preferred_element_type=F32)
            put(attn_q, mixed.astype(BF16))
            o = (dot_t(attn_w[3], wide(lambda i: attn_q[i])) + bias(3)).astype(BF16).astype(F32)
            for i in range(height):
                y = (feat[0, t, i].astype(F32) + o[:, i * width:(i + 1) * width]).astype(BF16)
                feat[0, t, i] = y
                xres[t, i] = y
            return 0

        lax.fori_loop(0, 2, frame, 0)

    x_copy().start()
    start_weights(0)
    barrier = pltpu.get_barrier_semaphore()
    for d in range(1, ranks):
        pl.semaphore_signal(barrier, inc=1, device_id={"time": lax.rem(me + d, ranks)}, device_id_type=MESH)
    start_weights(1)
    for s in range(4):
        for row in (0, height + 1):
            u_bufs[s][row] = jnp.zeros((k_tap, width), BF16)
    magic = (65536 + per_group - 1) // per_group
    r = lax.broadcasted_iota(jnp.int32, (channels, channels), 0) * magic // 65536
    c = lax.broadcasted_iota(jnp.int32, (channels, channels), 1) * magic // 65536
    member[...] = jnp.where(r == c, 1.0, 0.0).astype(BF16)
    x_copy().wait()
    for t in range(2):
        for i in range(height):
            x = x_in[t, pl.ds(i * width, width), :].T
            feat[0, t, i] = x
            xres[t, i] = x

    def plain_value(t, c0, i):
        return feat[0, t, i, pl.ds(c0, CHUNK), :].astype(F32)

    accumulate_stats(plain_value)
    pl.semaphore_wait(barrier, ranks - 1)
    send_stats(0)
    start_halo(0)

    def conv_stage(k, _):
        src = k % 2
        dst = 1 - src
        n = k + k // 2
        slot = k % 2
        bias_col[...] = column(conv_b[pl.ds(k, 1), :])
        norm_coefs(n)
        fill_u(frame_read(src, 0), 2)
        wait_weights(k, 2)
        wait_weights(k, 1)
        put(acc.at[0], dot_t(weights(slot, 2), taps(2)))
        for c0 in range(0, channels, CHUNK):
            fill_rows(frame_read(src, 1), 3, c0, CHUNK)
        put(acc.at[1], dot_t(weights(slot, 1, 2), jnp.concatenate([taps(2), taps(3)], axis=0)))
        wait_weights(k, 0)
        get_halo(k, 1)
        put(acc.at[1], wide(lambda i: acc[1, i]) + dot_t(weights(slot, 0), taps(1)))
        put(acc.at[0], wide(lambda i: acc[0, i]) + dot_t(weights(slot, 1), taps(1)))
        get_halo(k, 0)

        @pl.when(me < ranks - 1)
        def _():
            for t in (1, 0):
                halo_copy(k, t).wait_send()

        odd = src == 1

        def finish(t, value):
            for c0 in range(0, channels, CHUNK):
                rows = pl.ds(c0, CHUNK)
                s1 = jnp.zeros((CHUNK, width), F32) if t else part[0, rows, :]
                s2 = jnp.zeros((CHUNK, width), F32) if t else part[1, rows, :]
                ys = []
                for i in range(height):
                    h = (value(i, c0) + bias_col[rows, :]).astype(BF16).astype(F32)
                    y = jnp.where(odd, xres[t, i, rows, :].astype(F32) + h, h).astype(BF16)
                    ys.append(y)
                    y = y.astype(F32)
                    s1 = s1 + y
                    s2 = s2 + y * y
                for i in range(height):
                    feat[dst, t, i, rows, :] = ys[i]
                part[0, rows, :] = s1
                part[1, rows, :] = s2

        last = dot_t(weights(slot, 0), taps(0))
        finish(1, lambda i, c0: acc[1, i, pl.ds(c0, CHUNK), :])
        finish(0, lambda i, c0: acc[0, i, pl.ds(c0, CHUNK), :]
               + last[c0:c0 + CHUNK, i * width:(i + 1) * width])

        @pl.when(k < 2)
        def _():
            start_weights(k + 2)

        @pl.when(k < 3)
        def _():
            send_stats(n + 1)

        @pl.when(src == 0)
        def _():
            start_halo(k + 1)

        @pl.when(k == 1)
        def _():
            norm_coefs(2)
            attention()
            accumulate_stats(plain_value)
            send_stats(3)
            start_halo(2)

        return 0

    lax.fori_loop(0, 4, conv_stage, 0)
    for t in range(2):
        for i in range(height):
            out_ref[t, pl.ds(i * width, width), :] = feat[0, t, i].T


def solution(mesh):
    ranks = mesh.shape["time"]
    video_spec = P(("batch", "time"), None, None, None)

    def device_body(latent, conv_w, conv_b, norm_g, norm_b, attn_w, attn_b):
        frames, height, width, channels = latent.shape
        npos = height * width
        vmem = pl.BlockSpec(memory_space=pltpu.VMEM)
        hbm = pl.BlockSpec(memory_space=pl.ANY)
        dma = pltpu.SemaphoreType.DMA
        out = pl.pallas_call(
            functools.partial(kernel, ranks, height, width),
            out_shape=jax.ShapeDtypeStruct((frames, npos, channels), BF16),
            in_specs=[hbm, hbm] + [vmem] * 5,
            out_specs=vmem,
            scratch_shapes=[
                pltpu.VMEM((frames, npos, channels), BF16),
                pltpu.VMEM((2, 3, channels // 128, 9 * channels, 128), BF16),
                pltpu.VMEM((height + 2, 3 * channels, width), BF16),
                pltpu.VMEM((height + 2, 3 * channels, width), BF16),
                pltpu.VMEM((height + 2, 3 * channels, width), BF16),
                pltpu.VMEM((height + 2, 3 * channels, width), BF16),
                pltpu.VMEM((2, height, channels, width), F32),
                pltpu.VMEM((2, 2, height, channels, width), BF16),
                pltpu.VMEM((2, height, channels, width), BF16),
                pltpu.VMEM((4, 2, height, channels, width), BF16),
                pltpu.VMEM((2, channels, 128), F32),
                pltpu.VMEM((5, ranks, 2, channels), F32),
                pltpu.VMEM((3, channels, 128), F32),
                pltpu.VMEM((channels, 128), F32),
                pltpu.VMEM((channels, channels), BF16),
                pltpu.VMEM((2, height, channels, width), BF16),
                pltpu.VMEM((height, channels, width), BF16),
                pltpu.VMEM((height, channels, width), BF16),
                pltpu.VMEM((height, channels, width), BF16),
                pltpu.VMEM((height, npos, width), BF16),
                dma(()), dma((2, 3, channels // 128)), dma((5, ranks)), dma((5, ranks)), dma((4, 2)), dma((4, 2)),
            ],
            compiler_params=pltpu.CompilerParams(
                collective_id=0, has_side_effects=True, vmem_limit_bytes=62 * 2 ** 20),
            name="mid_block",
        )(latent.reshape(frames, npos, channels), conv_w.reshape(4, 3, 9 * channels, channels),
          conv_b, norm_g, norm_b, attn_w, attn_b)
        return out.reshape(latent.shape)

    return jax.shard_map(device_body, mesh=mesh, in_specs=(video_spec, P(), P(), P(), P(), P(), P()),
                         out_specs=video_spec, check_vma=False)
```

time: 119 us -> 107 us (0.90)
  Pallas kernels: 116 us -> 104 us
    pallas_call x1, Pallas kernels: 116 us -> 104 us  [device_body(): pl.pallas_call(functools.partial(kernel, ranks, height, width), out_shape...]
where the time goes in v1:
time: 107 us
  Pallas kernels  104 us (97%)
  local copies, waits for them, and re-layouts  2.41 us (2%)
    pallas_call x1, Pallas kernels, device_body(): pl.pallas_call(functools.partial(kernel, ranks, height, width), out_shape...  104 us
    unnamed x1, local copies, waits for them, and re-layouts  2.41 us

profile of v1, /device:TPU:81, one launch (start us, length us, event | category | flops | bytes accessed | tf_op | source)
XLA Modules:
  0.0 106.8 jit_solution(6485264962868677166)
XLA Ops:
  0.0 104.4 %mid_block.1 = bf16[2,768,384]{2,1,0:T(8,128)(2,1)} custom-call(bf16[2,768,384]{2,1,0:T(8,128)(2,1)} %bitcast.5, bf16[4,3,3456,384]{3,2,1,0:T(8,128)(2,1)} %bitcast.3, f32[4,384]{1,0:T(4,128)} %conv_b.1, f32[5,384]{1,0:T(8,128)} %norm_g.1, f32[5,384]{1,0:T(8,128)} %norm_b.1, bf16[4,384,384]{2,1,0:T(8,128)(2,1)} %attn_w.1, f32[4,384]{1,0:T(4,128)} %attn_b.1), custom_call_target="tpu_custom_call" | custom-call | tf_op jit(solution)/shard_map/mid_block/pallas_call | solution.py:321
  104.4 2.4 %copy.9 = bf16[2,6,128,384]{3,2,1,0:T(8,128)(2,1)} copy(bf16[2,6,128,384]{3,2,1,0:T(8,128)(2,1)} %bitcast.4) | data formatting | bytes 2359296

commit v2 on v1

--- a/solution.py
+++ b/solution.py
@@ -10,7 +10,6 @@
 GROUPS = 32
 NORM_EPS = 1e-6
 CHUNK = 64
-WIDE = 128
 MESH = pl.DeviceIdType.MESH
 F32 = jnp.float32
 BF16 = jnp.bfloat16
@@ -79,14 +78,14 @@
     def send_stats(n):
         rows = [jnp.sum(part[i].T, axis=0, keepdims=True) for i in range(2)]
         stat[n, me] = jnp.concatenate(rows, axis=0)
-        for d in range(1, ranks):
+        for d in sorted(range(1, ranks), key=lambda d: -min(d, ranks - d)):
             stat_copy(n, me, lax.rem(me + d, ranks)).start()
 
     def column(row):
         return jnp.broadcast_to(row, (128, channels)).T
 
-    def norm_coefs(n):
-        coef[2] = column(norm_b[pl.ds(n, 1), :])
+    def norm_coefs(n, factor):
+        coef[2] = column(norm_b[pl.ds(n, 1), :] * factor)
         for d in range(1, ranks):
             stat_copy(n, lax.rem(me + d, ranks), lax.rem(me + d, ranks)).wait_recv()
         totals = jnp.sum(stat[n], axis=0)
@@ -100,7 +99,7 @@
         sums = sums[0:8] + sums[8:16] + sums[16:24]
         mean = sums[0:1] / elem_count
         var = sums[1:2] / elem_count - mean * mean
-        scale = lax.rsqrt(var + NORM_EPS) * norm_g[pl.ds(n, 1), :]
+        scale = lax.rsqrt(var + NORM_EPS) * norm_g[pl.ds(n, 1), :] * factor
         coef[0] = column(mean)
         coef[1] = column(scale)
         for d in range(1, ranks):
@@ -113,7 +112,7 @@
     def fill_rows(read, s, c0, size):
         lane = lax.broadcasted_iota(jnp.int32, (size, width), 1)
         for i in range(height):
-            half = 0.5 * normalize(read(c0, size, i), c0, size)
+            half = normalize(read(c0, size, i), c0, size)
             u = (half + half * jnp.tanh(half)).astype(BF16)
             left = jnp.where(lane == 0, jnp.zeros_like(u), pltpu.roll(u, 1, 1))
             right = jnp.where(lane == width - 1, jnp.zeros_like(u), pltpu.roll(u, width - 1, 1))
@@ -121,11 +120,10 @@
                 u_bufs[s][i + 1, pl.ds(e * channels + c0, size), :] = v
 
     def fill_u(read, s):
-        def body(ci, _):
-            fill_rows(read, s, pl.multiple_of(ci * WIDE, WIDE), WIDE)
-            return 0
-
-        lax.fori_loop(0, channels // WIDE, body, 0)
+        @pl.when(me >= 0)
+        def _():
+            for c0 in range(0, channels, CHUNK):
+                fill_rows(read, s, c0, CHUNK)
 
     def taps(s):
         return jnp.concatenate([wide(lambda i: u_bufs[s][d + i]) for d in range(3)], axis=0)
@@ -236,7 +234,7 @@
         n = k + k // 2
         slot = k % 2
         bias_col[...] = column(conv_b[pl.ds(k, 1), :])
-        norm_coefs(n)
+        norm_coefs(n, 0.5)
         fill_u(frame_read(src, 0), 2)
         wait_weights(k, 2)
         wait_weights(k, 1)
@@ -294,7 +292,7 @@
 
         @pl.when(k == 1)
         def _():
-            norm_coefs(2)
+            norm_coefs(2, 1.0)
             attention()
             accumulate_stats(plain_value)
             send_stats(3)

time: 107 us -> 104 us (0.972)
  Pallas kernels: 104 us -> 101 us
    pallas_call x1, Pallas kernels: 104 us -> 101 us  [device_body(): pl.pallas_call(functools.partial(kernel, ranks, height, width), out_shape...]
where the time goes in v2:
time: 104 us
  Pallas kernels  101 us (97%)
  local copies, waits for them, and re-layouts  2.41 us (2%)
    pallas_call x1, Pallas kernels, device_body(): pl.pallas_call(functools.partial(kernel, ranks, height, width), out_shape...  101 us
    unnamed x1, local copies, waits for them, and re-layouts  2.41 us

profile of v2, /device:TPU:81, one launch (start us, length us, event | category | flops | bytes accessed | tf_op | source)
XLA Modules:
  0.0 103.6 jit_solution(10356362216167369689)
XLA Ops:
  0.0 101.2 %mid_block.1 = bf16[2,768,384]{2,1,0:T(8,128)(2,1)} custom-call(bf16[2,768,384]{2,1,0:T(8,128)(2,1)} %bitcast.5, bf16[4,3,3456,384]{3,2,1,0:T(8,128)(2,1)} %bitcast.3, f32[4,384]{1,0:T(4,128)} %conv_b.1, f32[5,384]{1,0:T(8,128)} %norm_g.1, f32[5,384]{1,0:T(8,128)} %norm_b.1, bf16[4,384,384]{2,1,0:T(8,128)(2,1)} %attn_w.1, f32[4,384]{1,0:T(4,128)} %attn_b.1), custom_call_target="tpu_custom_call" | custom-call | tf_op jit(solution)/shard_map/mid_block/pallas_call | solution.py:319
  101.2 2.4 %copy.9 = bf16[2,6,128,384]{3,2,1,0:T(8,128)(2,1)} copy(bf16[2,6,128,384]{3,2,1,0:T(8,128)(2,1)} %bitcast.4) | data formatting | bytes 2359296

commit v3 on v2

--- a/solution.py
+++ b/solution.py
@@ -19,10 +19,11 @@
     return lax.dot_general(lhs, rhs, (((0,), (0,)), ((), ())), preferred_element_type=F32)
 
 
-def kernel(ranks, height, width, x_hbm, w_hbm, conv_b, norm_g, norm_b, attn_w, attn_b, out_ref,
+def kernel(ranks, height, width, x_hbm, w_hbm, conv_b_hbm, norm_g_hbm, norm_b_hbm, attn_w_hbm, attn_b_hbm, out_hbm,
+           conv_b, norm_g, norm_b, attn_w, attn_b,
            x_in, w_buf, u_0, u_1, u_2, u_3, acc, feat, xres, halo, part, stat, coef, bias_col, member,
            attn_a, attn_q, attn_k, attn_v, attn_p,
-           x_sem, w_sem, stat_send, stat_recv, halo_send, halo_recv):
+           x_sem, param_sem, out_sem, w_sem, stat_send, stat_recv, halo_send, halo_recv):
     me = lax.axis_index("time")
     channels = feat.shape[3]
     u_bufs = (u_0, u_1, u_2, u_3)
@@ -58,6 +59,12 @@
     def put(ref, value):
         for i in range(height):
             ref[i] = value[:, i * width:(i + 1) * width]
+
+    params = ((conv_b_hbm, conv_b), (norm_g_hbm, norm_g), (norm_b_hbm, norm_b), (attn_b_hbm, attn_b),
+              (attn_w_hbm, attn_w))
+
+    def param_copy(j):
+        return pltpu.make_async_copy(params[j][0], params[j][1], param_sem.at[j])
 
     def stat_copy(n, source, target):
         return pltpu.make_async_remote_copy(
@@ -201,7 +208,10 @@
         lax.fori_loop(0, 2, frame, 0)
 
     x_copy().start()
+    for j in range(4):
+        param_copy(j).start()
     start_weights(0)
+    param_copy(4).start()
     barrier = pltpu.get_barrier_semaphore()
     for d in range(1, ranks):
         pl.semaphore_signal(barrier, inc=1, device_id={"time": lax.rem(me + d, ranks)}, device_id_type=MESH)
@@ -224,6 +234,8 @@
         return feat[0, t, i, pl.ds(c0, CHUNK), :].astype(F32)
 
     accumulate_stats(plain_value)
+    for j in range(5):
+        param_copy(j).wait()
     pl.semaphore_wait(barrier, ranks - 1)
     send_stats(0)
     start_halo(0)
@@ -301,9 +313,15 @@
         return 0
 
     lax.fori_loop(0, 4, conv_stage, 0)
-    for t in range(2):
+    def out_copy(t):
+        return pltpu.make_async_copy(x_in.at[t], out_hbm.at[t], out_sem.at[t])
+
+    for t in (1, 0):
         for i in range(height):
-            out_ref[t, pl.ds(i * width, width), :] = feat[0, t, i].T
+            x_in[t, pl.ds(i * width, width), :] = feat[0, t, i].T
+        out_copy(t).start()
+    for t in (1, 0):
+        out_copy(t).wait()
 
 
 def solution(mesh):
@@ -313,15 +331,19 @@
     def device_body(latent, conv_w, conv_b, norm_g, norm_b, attn_w, attn_b):
         frames, height, width, channels = latent.shape
         npos = height * width
-        vmem = pl.BlockSpec(memory_space=pltpu.VMEM)
         hbm = pl.BlockSpec(memory_space=pl.ANY)
         dma = pltpu.SemaphoreType.DMA
         out = pl.pallas_call(
             functools.partial(kernel, ranks, height, width),
             out_shape=jax.ShapeDtypeStruct((frames, npos, channels), BF16),
-            in_specs=[hbm, hbm] + [vmem] * 5,
-            out_specs=vmem,
+            in_specs=[hbm] * 7,
+            out_specs=hbm,
             scratch_shapes=[
+                pltpu.VMEM(conv_b.shape, conv_b.dtype),
+                pltpu.VMEM(norm_g.shape, norm_g.dtype),
+                pltpu.VMEM(norm_b.shape, norm_b.dtype),
+                pltpu.VMEM(attn_w.shape, attn_w.dtype),
+                pltpu.VMEM(attn_b.shape, attn_b.dtype),
                 pltpu.VMEM((frames, npos, channels), BF16),
                 pltpu.VMEM((2, 3, channels // 128, 9 * channels, 128), BF16),
                 pltpu.VMEM((height + 2, 3 * channels, width), BF16),
@@ -342,7 +364,7 @@
                 pltpu.VMEM((height, channels, width), BF16),
                 pltpu.VMEM((height, channels, width), BF16),
                 pltpu.VMEM((height, npos, width), BF16),
-                dma(()), dma((2, 3, channels // 128)), dma((5, ranks)), dma((5, ranks)), dma((4, 2)), dma((4, 2)),
+                dma(()), dma((5,)), dma((2,)), dma((2, 3, channels // 128)), dma((5, ranks)), dma((5, ranks)), dma((4, 2)), dma((4, 2)),
             ],
             compiler_params=pltpu.CompilerParams(
                 collective_id=0, has_side_effects=True, vmem_limit_bytes=62 * 2 ** 20),

time: 104 us -> 102 us (0.981)
    pallas_call x1, Pallas kernels: 101 us -> 100 us  [device_body(): pl.pallas_call(functools.partial(kernel, ranks, height, width), out_shape...]
where the time goes in v3:
time: 102 us
  Pallas kernels  100 us (98%)
  local copies, waits for them, and re-layouts  2.41 us (2%)
    pallas_call x1, Pallas kernels, device_body(): pl.pallas_call(functools.partial(kernel, ranks, height, width), out_shape...  100 us
    unnamed x1, local copies, waits for them, and re-layouts  2.41 us

profile of v3, /device:TPU:81, one launch (start us, length us, event | category | flops | bytes accessed | tf_op | source)
XLA Modules:
  0.0 102.4 jit_solution(13756766020071468700)
XLA Ops:
  0.0 100.0 %mid_block.1 = bf16[2,768,384]{2,1,0:T(8,128)(2,1)} custom-call(bf16[2,768,384]{2,1,0:T(8,128)(2,1)} %bitcast.5, bf16[4,3,3456,384]{3,2,1,0:T(8,128)(2,1)} %bitcast.3, f32[4,384]{1,0:T(4,128)} %conv_b_hbm.1, f32[5,384]{1,0:T(8,128)} %norm_g_hbm.1, f32[5,384]{1,0:T(8,128)} %norm_b_hbm.1, bf16[4,384,384]{2,1,0:T(8,128)(2,1)} %attn_w_hbm.1, f32[4,384]{1,0:T(4,128)} %attn_b_hbm.1), custom_call_target="tpu_custom_call" | custom-call | tf_op jit(solution)/shard_map/mid_block/pallas_call | solution.py:336
  100.0 2.4 %copy.9 = bf16[2,6,128,384]{3,2,1,0:T(8,128)(2,1)} copy(bf16[2,6,128,384]{3,2,1,0:T(8,128)(2,1)} %bitcast.4) | data formatting | bytes 2359296
